TPU v7x, 256 devices: a whole 4x4x8 slice. The times are simulated.
256 devices in a mesh: dp: 16 (over x, z_lo), owner: 16 (over z_hi, y, core).
Axes of the slice: x: 4, y: 4, z: 8 (z_hi: 2, z_lo: 4; z = z_hi * 4 + z_lo), core: 2. Of those that a mesh axis runs over, the one named last changes fastest.
Arguments:
- layer_input: bfloat16 [4096, 8192], P('dp', 'owner'), may hold values from -6 to 6
- output_grads: bfloat16 [4096, 10240], P('dp', 'owner'), may hold values from -6 to 6
- projection: bfloat16 [8192, 10240], P('owner', 'dp'), may hold values from -0.0625 to 0.0625
Outputs:
- grad_input: bfloat16 [4096, 8192], P('dp', 'owner')
- update_query: bfloat16 [8192, 8192], P('owner', 'dp')
- update_kv: bfloat16 [8192, 2048], P('owner', 'dp')
All inputs are finite; a program needn't handle non-finite values.
Results may differ from a plain program's by a relative error of at most 0.023.
Values may be sent and summed in bfloat16 or wider, within the bound.
A program may use at most 128 MiB of HBM per device.

v0:
```python
import math
import jax
import jax.numpy as jnp
from jax import lax
from jax.sharding import Mesh
from jax.sharding import PartitionSpec as P

BLOCK = 512
QW = 8192
DP = ("dp_0", "dp_1")


def gather_axes(shard, axes, dim):
    whole = shard
    for number in range(len(axes) - 1, -1, -1):
        whole = lax.all_gather(whole, axes[number], axis=dim, tiled=True)
    return whole


def split_up(shard, dim, devices):
    before, after = (shard.shape[:dim], shard.shape[dim + 1 :])
    return jnp.moveaxis(shard.reshape(*before, devices, -1, *after), dim, 0)


def sum_at_owner(shard, axis, dim):
    devices = lax.axis_size(axis)
    blocks = lax.all_to_all(split_up(shard, dim, devices), axis, 0, 0, tiled=True)
    return jnp.sum(blocks.astype(jnp.float32), axis=0)


def left_stat(blocks):
    return jnp.einsum("...ij,...kj->...ik", blocks, blocks, preferred_element_type=jnp.float32)


def right_stat(blocks):
    return jnp.einsum("...ji,...jk->...ik", blocks, blocks, preferred_element_type=jnp.float32)


def inverse_root(statistic):
    width = statistic.shape[-1]
    scale = math.sqrt(width) * jnp.sqrt(
        jnp.mean(statistic * statistic, axis=(-2, -1), keepdims=True) + 1e-06
    )
    normed = statistic / scale
    identity = jnp.eye(width, dtype=jnp.float32)
    return scale ** (-0.25) * (5.0 * identity - normed) * 0.25


def left_finish(square, received):
    width = square.shape[-1]
    root_left = inverse_root(left_stat(square))
    whole = jnp.einsum("...ij,...jk->...ik", root_left, received, precision=lax.Precision.HIGHEST)
    return (whole * math.sqrt(width)).astype(jnp.bfloat16)


def precondition(blocks):
    root_right = inverse_root(right_stat(blocks))
    half = jnp.einsum(
        "...ij,...jk->...ik",
        blocks.astype(jnp.float32),
        root_right,
        precision=lax.Precision.HIGHEST,
    )
    return left_finish(blocks, half)


def place_block(buffer, result, row_start, col_start):
    return lax.dynamic_update_slice(buffer, result, (row_start, col_start))


def body(layer_input, output_grads, projection):
    width = BLOCK
    rows_own = layer_input.shape[1]
    gathered = lax.all_gather(output_grads, "owner", axis=1, tiled=True)
    section = gathered
    input_sum = jnp.einsum(
        "tc,rc->tr", section, gather_axes(projection, DP, 1), preferred_element_type=jnp.float32
    )
    grad_input = input_sum.astype(jnp.bfloat16)
    section = lax.slice_in_dim(gathered, 0, QW // lax.axis_size(DP) * lax.axis_size(DP), axis=1)
    query_local = lax.psum_scatter(
        jnp.einsum("tc,tr->cr", section, layer_input, preferred_element_type=jnp.float32).astype(
            jnp.bfloat16
        ),
        DP,
        scatter_dimension=0,
        tiled=True,
    )
    query_count = query_local.shape[0] // width
    row_count = rows_own // width
    shaped = query_local.reshape(query_count, width, row_count, width)
    squares = jnp.transpose(shaped, (2, 0, 3, 1)).reshape(row_count * query_count, width, width)
    updates = precondition(squares)
    update_query = jnp.transpose(
        updates.reshape(row_count, query_count, width, width), (0, 2, 1, 3)
    ).reshape(rows_own, query_count * width)
    kv_term = jnp.einsum(
        "tc,tr->cr", gathered[:, QW:], layer_input, preferred_element_type=jnp.float32
    )
    kv_grads = lax.psum(kv_term.astype(jnp.bfloat16), DP)
    kv_count = kv_grads.shape[0] // width
    total = row_count * kv_count
    index_dp = lax.axis_index(DP)
    buffer = jnp.zeros((rows_own, kv_grads.shape[0]), jnp.float32)
    empty_square = jnp.zeros((width, width), jnp.float32)
    number = 0 + index_dp
    valid = number < total
    clamped = jnp.minimum(number, total - 1)
    block_row = clamped // kv_count
    block_col = clamped % kv_count
    square = lax.dynamic_slice(kv_grads, (block_col * width, block_row * width), (width, width)).T
    square, row_start, col_start = (square, block_row * width, block_col * width)
    result = lax.cond(
        valid,
        lambda operand: precondition(operand).astype(jnp.float32),
        lambda operand: empty_square,
        square,
    )
    buffer = place_block(buffer, result, row_start, col_start)
    update_kv = sum_at_owner(buffer.astype(jnp.bfloat16), DP, 1).astype(jnp.bfloat16)
    return (grad_input, update_query, update_kv)


def solution(mesh):
    torus = Mesh(mesh.devices.reshape(4, 4, mesh.shape["owner"]), ("dp_0", "dp_1", "owner"))
    placed = (P(DP, "owner"), P(DP, "owner"), P("owner", DP))
    return jax.shard_map(
        body,
        mesh=torus,
        in_specs=placed,
        out_specs=(P(DP, "owner"), P("owner", DP), P("owner", DP)),
        check_vma=False,
    )
```

profile of v0, /device:TPU:1, one launch (start us, length us, event | category | flops | bytes accessed | tf_op | source)
XLA Modules:
  0.0 656.7 jit_solution(5530023113139257753)
XLA Ops:
  7.2 0.0 copy-start
  7.2 0.0 all-gather.4.cloned.1.call-start
  7.2 0.7 all-gather.4.cloned.1.call-update
  7.9 0.0 all-gather.6.cloned.1.call-start
  8.0 0.7 all-gather.6.cloned.1.call-update
  8.7 0.0 all-reduce.2.cloned.1.call-start
  8.7 91.2 %all-gather.4.cloned.1.call-done = bf16[256,10240]{1,0:T(8,128)(2,1)} async-done(((bf16[256,640]{1,0:T(8,128)(2,1)}), bf16[256,10240]{1,0:T(8,128)(2,1)}) %all-gather.4.cloned.1.call-update) | async-done | bytes 5242896 | tf_op jit(solution)/shard_map/all_gather | solution.py:74
  99.9 0.0 copy-done
  99.9 3.4 convolution_convert_fusion.1
  103.3 0.0 all-reduce.2.cloned.1.call-update
  103.3 0.0 all-gather.8.cloned.1.call-start
  103.4 51.8 %all-gather.6.cloned.1.call-done = bf16[512,2560]{1,0:T(8,128)(2,1)} async-done(((bf16[512,640]{1,0:T(8,128)(2,1)}), bf16[512,2560]{1,0:T(8,128)(2,1)}) %all-gather.6.cloned.1.call-update) | async-done | bytes 2621456 | tf_op jit(solution)/shard_map/all_gather | solution.py:16
  155.2 0.0 all-gather.8.cloned.1.call-update
  155.2 0.0 reduce-scatter.2.cloned.1.call-start
  155.2 7.9 %convolution_convert_fusion = bf16[8192,512]{1,0:T(8,128)(2,1)} fusion(bf16[256,512]{1,0:T(8,128)(2,1)S(1)} %copy-done, bf16[256,10240]{1,0:T(8,128)(2,1)} %all-gather.4.cloned.1.call-done), kind=kOutput, calls=%fused_computation.31 | convolution fusion | flops 2151677952 | bytes 12845056 | tf_op jit(solution)/shard_map/tc,tr->cr/dot_general | solution.py:82
  163.1 0.0 reduce-scatter.2.cloned.1.call-update
  163.2 161.2 %all-reduce.2.cloned.1.call-done = bf16[2048,512]{1,0:T(8,128)(2,1)} async-done(((bf16[2048,512]{1,0:T(8,128)(2,1)}), bf16[2048,512]{1,0:T(8,128)(2,1)}) %all-reduce.2.cloned.1.call-update) | async-done | bytes 2097168 | tf_op jit(solution)/shard_map/psum | solution.py:100
  324.4 1.1 dynamic-slice_bitcast_fusion
  325.5 7.2 %conditional.1 = (bf16[512,512]{0,1:T(8,128)(2,1)S(1)}) conditional(s32[]{:T(128)} %convert_element_type.36, () %tuple.14, bf16[512,512]{0,1:T(8,128)(2,1)S(1)} %dynamic-slice_bitcast_fusion), branch_computations={%region_4.5_spmd, %region_5.8_spmd} | conditional | flops 3762814976 | bytes 9437328 | solution.py:113
  325.5 1.2 multiply_reduce_fusion
  327.4 1.1 fusion.7
  328.5 1.2 multiply_reduce_fusion.1
  330.4 2.0 fusion.1
  332.4 0.2 copy.13
  332.7 0.1 broadcast_in_dim.4
  332.9 2.4 copy.10
  335.3 50.0 %all_to_all.5 = bf16[16,512,128]{2,1,0:T(8,128)(2,1)S(1)} all-to-all(bf16[16,512,128]{2,1,0:T(8,128)(2,1)} %copy.10), channel_id=1, replica_groups=mesh['dp_0'=4,'dp_1'=4,'owner'=16] {'dp_0','dp_1'}, dimensions={0} | all-to-all | bytes 4194304 | tf_op jit(solution)/shard_map/all_to_all | solution.py:27
  385.3 1.0 reduce_sum.50
  386.2 65.5 %all-gather.8.cloned.1.call-done = bf16[512,10240]{1,0:T(8,128)(2,1)} async-done(((bf16[512,2560]{1,0:T(8,128)(2,1)}), bf16[512,10240]{1,0:T(8,128)(2,1)}) %all-gather.8.cloned.1.call-update) | async-done | bytes 10485776 | tf_op jit(solution)/shard_map/all_gather | solution.py:16
  451.7 9.2 %convolution_convert_fusion.2 = bf16[256,512]{1,0:T(8,128)(2,1)} fusion(bf16[256,10240]{1,0:T(8,128)(2,1)} %all-gather.4.cloned.1.call-done, bf16[512,10240]{1,0:T(8,128)(2,1)} %all-gather.8.cloned.1.call-done), kind=kOutput, calls=%fused_computation.38 | convolution fusion | flops 2684485632 | bytes 15990784 | tf_op jit(solution)/shard_map/tc,rc->tr/dot_general | solution.py:76
  460.9 178.0 %reduce-scatter.2.cloned.1.call-done = bf16[512,512]{1,0:T(8,128)(2,1)} async-done(((bf16[8192,512]{1,0:T(8,128)(2,1)}), bf16[512,512]{1,0:T(8,128)(2,1)}) %reduce-scatter.2.cloned.1.call-update) | async-done | bytes 524304 | tf_op jit(solution)/shard_map/reduce_scatter | solution.py:81
  638.8 2.4 multiply_reduce_fusion.2
  641.9 2.4 multiply_reduce_fusion.3
  645.2 2.3 fusion.34
  647.4 2.8 fusion.28
  (1 shorter events, 0.0 us)
Async XLA Ops:
  7.2 92.8 %copy-start = (bf16[256,512]{1,0:T(8,128)(2,1)S(1)}, bf16[256,512]{1,0:T(8,128)(2,1)}, u32[]{:S(2)}) copy-start(bf16[256,512]{1,0:T(8,128)(2,1)} %param.5) | copy-start | bytes 786436
  7.2 92.8 %all-gather.4.cloned.1.call-start = ((), (), s32[]{:S(2)}) async-start(), calls=%async_computation.2 | async-start | bytes 5570560 | tf_op jit(solution)/shard_map/all_gather | solution.py:74
  7.9 147.2 %all-gather.6.cloned.1.call-start = ((), (), s32[]{:S(2)}) async-start(), calls=%async_computation.3 | async-start | bytes 3276800 | tf_op jit(solution)/shard_map/all_gather | solution.py:16
  8.7 315.7 %all-reduce.2.cloned.1.call-start = ((), (), s32[]{:S(2)}) async-start(), calls=%async_computation.6 | async-start | bytes 4194304 | tf_op jit(solution)/shard_map/psum | solution.py:100
  103.3 348.4 %all-gather.8.cloned.1.call-start = ((), (), s32[]{:S(2)}) async-start(), calls=%async_computation.4 | async-start | bytes 13107200 | tf_op jit(solution)/shard_map/all_gather | solution.py:16
  155.2 483.7 %reduce-scatter.2.cloned.1.call-start = ((), (), s32[]{:S(2)}) async-start(), calls=%async_computation.5 | async-start | bytes 8912896 | tf_op jit(solution)/shard_map/reduce_scatter | solution.py:81
Sparse Core Ops, SparseCore 0:
  10.7 89.1 all-gather.3
  101.8 53.3 all-gather.5
  157.8 166.5 all-reduce.1
  326.0 125.6 all-gather.7
  454.1 184.6 reduce-scatter.1
where the time goes:
time: 657 us
  waiting for transfers between devices  549 us (84%)
  blocking collectives  50 us (8%)
  matrix products  35.8 us (5%)
  between operations  15.3 us (2%)
    reduce_scatter x1, waiting for transfers between devices, body(): lax.psum_scatter(jnp.einsum('tc,tr->cr', section, layer_input, preferred_...  178 us
    psum x1, waiting for transfers between devices, body(): kv_grads = lax.psum(kv_term.astype(jnp.bfloat16), DP)  161 us
    all_gather x2, waiting for transfers between devices, gather_axes(): whole = lax.all_gather(whole, axes[number], axis=dim, tiled=True)  117 us
    all_gather x1, waiting for transfers between devices, body(): gathered = lax.all_gather(output_grads, 'owner', axis=1, tiled=True)  91.2 us
    all_to_all x1, blocking collectives, sum_at_owner(): lax.all_to_all(split_up(shard, dim, devices), axis, 0, 0, tiled=True)  50 us
  transfers between devices with their start and end apart: 5, of which 5 were waited for; matrix products, arithmetic and copies ran while one was open for 5% of the time, Pallas kernels for 0%

commit v1 on v0

--- a/solution.py
+++ b/solution.py
@@ -97,7 +97,9 @@
     kv_term = jnp.einsum(
         "tc,tr->cr", gathered[:, QW:], layer_input, preferred_element_type=jnp.float32
     )
-    kv_grads = lax.psum(kv_term.astype(jnp.bfloat16), DP)
+    kv_grads = kv_term.astype(jnp.bfloat16)
+    for name in ("dp_0", "dp_1"):
+        kv_grads = lax.psum(kv_grads, name)
     kv_count = kv_grads.shape[0] // width
     total = row_count * kv_count
     index_dp = lax.axis_index(DP)

time: 657 us -> 509 us (0.77)
  waiting for transfers between devices: 549 us -> 351 us
  blocking collectives: 50 us -> 97.9 us
    all_gather x2, waiting for transfers between devices: 117 us -> 0.03 us  [gather_axes(): whole = lax.all_gather(whole, axes[number], axis=dim, tiled=True)]
    reduce_scatter x1, waiting for transfers between devices: 178 us -> 111 us  [body(): lax.psum_scatter(jnp.einsum('tc,tr->cr', section, layer_input, preferred_...]
    all_to_all x1, blocking collectives: 50 us -> 97.9 us  [sum_at_owner(): lax.all_to_all(split_up(shard, dim, devices), axis, 0, 0, tiled=True)]
    psum x1 -> x2, waiting for transfers between devices: 161 us -> 146 us  [body(): kv_grads = lax.psum(kv_grads, name)]
  transfers between devices with their start and end apart: 5 -> 6, of which waited for: 5 -> 4; matrix products, arithmetic and copies ran while one was open for 5% -> 5% of each run, Pallas kernels for 0% -> 0%
where the time goes in v1:
time: 509 us; the launch traced here: 508 us
  waiting for transfers between devices  351 us (69%)
  blocking collectives  97.9 us (19%)
  matrix products  35.8 us (7%)
  between operations  16.8 us (3%)
    psum x2, waiting for transfers between devices, body(): kv_grads = lax.psum(kv_grads, name)  146 us
    reduce_scatter x1, waiting for transfers between devices, body(): lax.psum_scatter(jnp.einsum('tc,tr->cr', section, layer_input, preferred_...  111 us
    all_to_all x1, blocking collectives, sum_at_owner(): lax.all_to_all(split_up(shard, dim, devices), axis, 0, 0, tiled=True)  97.9 us
    all_gather x1, waiting for transfers between devices, body(): gathered = lax.all_gather(output_grads, 'owner', axis=1, tiled=True)  92 us
  transfers between devices with their start and end apart: 6, of which 4 were waited for; matrix products, arithmetic and copies ran while one was open for 5% of the time, Pallas kernels for 0%

profile of v1, /device:TPU:1, one launch (start us, length us, event | category | flops | bytes accessed | tf_op | source)
XLA Modules:
  0.0 508.1 jit_solution(14772399127779316900)
XLA Ops:
  8.0 0.0 copy-start
  8.0 0.0 all-gather.4.cloned.1.call-start
  8.1 0.7 all-gather.4.cloned.1.call-update
  8.7 0.0 all-reduce.3.cloned.1.call-start
  8.8 92.0 %all-gather.4.cloned.1.call-done = bf16[256,10240]{1,0:T(8,128)(2,1)} async-done(((bf16[256,640]{1,0:T(8,128)(2,1)}), bf16[256,10240]{1,0:T(8,128)(2,1)}) %all-gather.4.cloned.1.call-update) | async-done | bytes 5242896 | tf_op jit(solution)/shard_map/all_gather | solution.py:74
  100.8 0.0 copy-done
  100.8 3.3 convolution_convert_fusion.1
  104.1 0.0 all-reduce.3.cloned.1.call-update
  104.1 0.0 all-gather.6.cloned.1.call-start
  104.2 0.5 all-gather.6.cloned.1.call-update
  104.7 0.0 all-reduce.5.cloned.1.call-start
  104.7 58.2 %all-reduce.3.cloned.1.call-done = bf16[2048,512]{1,0:T(8,128)(2,1)} async-done(((bf16[2048,512]{1,0:T(8,128)(2,1)}), bf16[2048,512]{1,0:T(8,128)(2,1)}) %all-reduce.3.cloned.1.call-update) | async-done | bytes 2097168 | tf_op jit(solution)/shard_map/psum | solution.py:102
  162.9 0.0 all-reduce.5.cloned.1.call-update
  163.0 0.0 all-gather.8.cloned.1.call-start
  163.0 0.0 all-gather.6.cloned.1.call-done
  163.1 0.6 all-gather.8.cloned.1.call-update
  163.7 0.0 reduce-scatter.2.cloned.1.call-start
  163.8 7.9 %convolution_convert_fusion = bf16[8192,512]{1,0:T(8,128)(2,1)} fusion(bf16[256,512]{1,0:T(8,128)(2,1)S(1)} %copy-done, bf16[256,10240]{1,0:T(8,128)(2,1)} %all-gather.4.cloned.1.call-done), kind=kOutput, calls=%fused_computation.31 | convolution fusion | flops 2151677952 | bytes 12845056 | tf_op jit(solution)/shard_map/tc,tr->cr/dot_general | solution.py:82
  171.7 0.0 reduce-scatter.2.cloned.1.call-update
  171.7 88.0 %all-reduce.5.cloned.1.call-done = bf16[2048,512]{1,0:T(8,128)(2,1)} async-done(((bf16[2048,512]{1,0:T(8,128)(2,1)}), bf16[2048,512]{1,0:T(8,128)(2,1)}) %all-reduce.5.cloned.1.call-update) | async-done | bytes 2097168 | tf_op jit(solution)/shard_map/psum | solution.py:102
  259.7 1.1 dynamic-slice_bitcast_fusion
  260.8 7.2 %conditional.1 = (bf16[512,512]{0,1:T(8,128)(2,1)S(1)}) conditional(s32[]{:T(128)} %convert_element_type.36, () %tuple.14, bf16[512,512]{0,1:T(8,128)(2,1)S(1)} %dynamic-slice_bitcast_fusion), branch_computations={%region_5.6_spmd, %region_6.9_spmd} | conditional | flops 3762814976 | bytes 9437328 | solution.py:115
  260.8 1.2 multiply_reduce_fusion
  262.7 1.1 fusion.7
  263.8 1.2 multiply_reduce_fusion.1
  265.8 2.0 fusion.1
  267.8 0.2 copy.13
  268.0 0.1 broadcast_in_dim.4
  268.2 2.4 copy.10
  270.6 97.9 %all_to_all.5 = bf16[16,512,128]{2,1,0:T(8,128)(2,1)S(1)} all-to-all(bf16[16,512,128]{2,1,0:T(8,128)(2,1)} %copy.10), channel_id=1, replica_groups=mesh['dp_0'=4,'dp_1'=4,'owner'=16] {'dp_0','dp_1'}, dimensions={0} | all-to-all | bytes 4194304 | tf_op jit(solution)/shard_map/all_to_all | solution.py:27
  368.5 1.0 reduce_sum.50
  369.5 0.0 all-gather.8.cloned.1.call-done
  369.5 9.3 %convolution_convert_fusion.2 = bf16[256,512]{1,0:T(8,128)(2,1)} fusion(bf16[256,10240]{1,0:T(8,128)(2,1)} %all-gather.4.cloned.1.call-done, bf16[512,10240]{1,0:T(8,128)(2,1)} %all-gather.8.cloned.1.call-done), kind=kOutput, calls=%fused_computation.38 | convolution fusion | flops 2684485632 | bytes 15990784 | tf_op jit(solution)/shard_map/tc,rc->tr/dot_general | solution.py:76
  378.7 110.8 %reduce-scatter.2.cloned.1.call-done = bf16[512,512]{1,0:T(8,128)(2,1)} async-done(((bf16[8192,512]{1,0:T(8,128)(2,1)}), bf16[512,512]{1,0:T(8,128)(2,1)}) %reduce-scatter.2.cloned.1.call-update) | async-done | bytes 524304 | tf_op jit(solution)/shard_map/reduce_scatter | solution.py:81
  489.6 2.4 multiply_reduce_fusion.2
  492.7 2.4 multiply_reduce_fusion.3
  495.9 2.3 fusion.34
  498.2 2.8 fusion.28
  (1 shorter events, 0.0 us)
Async XLA Ops:
  8.0 92.8 %copy-start = (bf16[256,512]{1,0:T(8,128)(2,1)S(1)}, bf16[256,512]{1,0:T(8,128)(2,1)}, u32[]{:S(2)}) copy-start(bf16[256,512]{1,0:T(8,128)(2,1)} %param.5) | copy-start | bytes 786436
  8.0 92.8 %all-gather.4.cloned.1.call-start = ((), (), s32[]{:S(2)}) async-start(), calls=%async_computation.2 | async-start | bytes 5570560 | tf_op jit(solution)/shard_map/all_gather | solution.py:74
  8.7 154.2 %all-reduce.3.cloned.1.call-start = ((), (), s32[]{:S(2)}) async-start(), calls=%async_computation.6 | async-start | bytes 4194304 | tf_op jit(solution)/shard_map/psum | solution.py:102
  104.1 58.9 %all-gather.6.cloned.1.call-start = ((), (), s32[]{:S(2)}) async-start(), calls=%async_computation.3 | async-start | bytes 3276800 | tf_op jit(solution)/shard_map/all_gather | solution.py:16
  104.7 155.0 %all-reduce.5.cloned.1.call-start = ((), (), s32[]{:S(2)}) async-start(), calls=%async_computation.7 | async-start | bytes 4194304 | tf_op jit(solution)/shard_map/psum | solution.py:102
  163.0 206.5 %all-gather.8.cloned.1.call-start = ((), (), s32[]{:S(2)}) async-start(), calls=%async_computation.4 | async-start | bytes 13107200 | tf_op jit(solution)/shard_map/all_gather | solution.py:16
  163.7 325.9 %reduce-scatter.2.cloned.1.call-start = ((), (), s32[]{:S(2)}) async-start(), calls=%async_computation.5 | async-start | bytes 8912896 | tf_op jit(solution)/shard_map/reduce_scatter | solution.py:81
Sparse Core Ops, SparseCore 0:
  11.6 89.1 all-gather.3
  104.2 58.6 all-reduce.2
  165.6 103.1 all-gather.7
  271.2 218.3 reduce-scatter.1
Sparse Core Ops, SparseCore 1:
  106.4 53.1 all-gather.5
  163.1 96.6 all-reduce.4
